TPU v7x, 32 devices: a whole 2x2x4 slice. The times are simulated.
32 devices in a mesh: replica: 4 (over x, core), fsdp: 8 (over z, y).
Axes of the slice: x: 2, y: 2, z: 4, core: 2. Of those that a mesh axis runs over, the one named last changes fastest.
Arguments:
- deltas: bfloat16 [4, 2, 2048, 16384], P('replica', None, 'fsdp'), may hold values from -3 to 3
- master: float32 [2, 2048, 16384], P(None, 'replica', 'fsdp'), may hold values from -3 to 3
- momentum: float32 [2, 2048, 16384], P(None, 'replica', 'fsdp'), may hold values from -2 to 2
Outputs:
- master_out: float32 [2, 2048, 16384], P(None, 'replica', 'fsdp')
- momentum_out: float32 [2, 2048, 16384], P(None, 'replica', 'fsdp')
- params_out: bfloat16 [2, 2048, 16384], P(None, 'fsdp')
All inputs are finite; a program needn't handle non-finite values.
Results may differ from a plain program's by a relative error of at most 0.008.
Values may be sent and summed in bfloat16 or wider, within the bound.
A program may use at most 128 MiB of HBM per device.

v0:
```python
import jax
import jax.numpy as jnp
from jax import lax
from jax.sharding import PartitionSpec as P


def on_device(deltas, master, momentum):
    local = deltas[0]
    groups = lax.axis_size("replica")
    moved = lax.all_to_all(local, "fsdp", split_axis=2, concat_axis=1, tiled=True)
    summed = lax.psum_scatter(
        moved.astype(jnp.float32).astype(jnp.bfloat16), "replica", scatter_dimension=1, tiled=True
    ).astype(jnp.float32)
    outer = summed / groups
    velocity = 0.9 * momentum + outer
    updated = master - 0.7 * (outer + 0.9 * velocity)
    rounded = updated.astype(jnp.bfloat16)
    copies = lax.all_gather(rounded, "replica", axis=1, tiled=True)
    spread = lax.all_to_all(copies, "fsdp", split_axis=1, concat_axis=2, tiled=True)
    return (updated, velocity, spread)


def solution(mesh):
    return jax.shard_map(
        on_device,
        mesh=mesh,
        in_specs=(
            P("replica", None, "fsdp", None),
            P(None, "replica", "fsdp"),
            P(None, "replica", "fsdp"),
        ),
        out_specs=(P(None, "replica", "fsdp"), P(None, "replica", "fsdp"), P(None, "fsdp", None)),
        check_vma=False,
    )
```

profile of v0, /device:TPU:0, one launch (start us, length us, event | category | flops | bytes accessed | tf_op | source)
XLA Modules:
  0.0 1325.4 jit_solution(8873194051052167290)
XLA Ops:
  7.2 0.0 all-reduce.3.cloned.1.call-start
  7.2 40.8 %copy.22 = bf16[1,2,256,16384]{2,1,3,0:T(2,128)(2,1)} copy(bf16[1,2,256,16384]{3,2,1,0:T(8,128)(2,1)} %param.3) | data formatting | bytes 33554432 | tf_op args[0]
  48.0 372.0 %all_to_all.36 = bf16[2,256,16384]{1,0,2:T(2,128)(2,1)} all-to-all(bf16[2,256,16384]{1,0,2:T(2,128)(2,1)} %bitcast.14), channel_id=1, replica_groups=mesh['replica'=4,'fsdp'=8] {'fsdp'}, dimensions={2} | all-to-all | bytes 33554432 | tf_op jit(solution)/shard_map/all_to_all | solution.py:10
  420.0 60.3 %copy.23 = bf16[2,8,256,2048]{3,0,2,1:T(2,128)(2,1)} copy(bf16[2,8,256,2048]{2,0,3,1:T(2,128)(2,1)} %bitcast.12) | data formatting | bytes 33554432 | tf_op jit(solution)/shard_map/all_to_all | solution.py:10
  480.3 0.0 copy-start
  480.3 0.0 all-reduce.3.cloned.1.call-update
  480.3 0.0 all-gather.2.cloned.1.call-start
  480.4 0.6 copy-done
  481.0 0.6 dynamic-slice
  482.2 285.7 %all-reduce.3.cloned.1.call-done = bf16[2,2048,2048]{2,0,1:T(2,128)(2,1)} async-done(((bf16[2,2048,2048]{2,0,1:T(2,128)(2,1)}), bf16[2,2048,2048]{2,0,1:T(2,128)(2,1)}) %all-reduce.3.cloned.1.call-update) | async-done | bytes 16777232
  767.9 5.1 constant_dynamic-slice_fusion
  773.0 13.9 %fusion = (bf16[2,512,2048]{2,1,0:T(8,128)(2,1)}, f32[2,512,2048]{2,1,0:T(8,128)}, f32[2,512,2048]{2,1,0:T(8,128)}) fusion(f32[2,512,2048]{2,1,0:T(8,128)} %param.4, bf16[2,512,2048]{2,0,1:T(2,128)(2,1)S(1)} %constant_dynamic-slice_fusion, f32[2,512,2048]{2,1,0:T(8,128)} %param.5), kind=kLoop, calls=%fused_computation.4 | loop fusion | flops 18874368 | bytes 41943040 | tf_op jit(solution)/shard_map/convert_element_type | solution.py:17
  786.9 8.4 copy.25
  795.3 0.0 all-gather.2.cloned.1.call-update
  795.3 106.1 %all-gather.2.cloned.1.call-done = bf16[2,2048,2048]{2,0,1:T(2,128)(2,1)} async-done(((bf16[2,512,2048]{2,0,1:T(2,128)(2,1)}), bf16[2,2048,2048]{2,0,1:T(2,128)(2,1)}) %all-gather.2.cloned.1.call-update) | async-done | bytes 16777232 | tf_op jit(solution)/shard_map/all_gather | solution.py:18
  901.4 368.7 %all_to_all.37 = bf16[2,2048,2048]{2,0,1:T(2,128)(2,1)S(1)} all-to-all(bf16[2,2048,2048]{2,0,1:T(2,128)(2,1)} %all-gather.2.cloned.1.call-done), channel_id=1, replica_groups=mesh['replica'=4,'fsdp'=8] {'fsdp'}, dimensions={1} | all-to-all | bytes 33554432 | tf_op jit(solution)/shard_map/all_to_all | solution.py:19
  1270.1 22.9 %copy.26 = bf16[2,256,8,2048]{3,2,1,0:T(8,128)(2,1)} copy(bf16[2,256,8,2048]{3,0,1,2:T(2,128)(2,1)S(1)} %bitcast.13) | data formatting | bytes 33554432 | tf_op jit(solution)/shard_map/all_to_all | solution.py:19
  1293.0 25.5 %all_to_all.33 = bf16[2,256,16384]{2,1,0:T(8,128)(2,1)} reshape(bf16[2,256,8,2048]{3,2,1,0:T(8,128)(2,1)} %copy.26) | data formatting | bytes 33554432 | tf_op jit(solution)/shard_map/all_to_all | solution.py:19
Async XLA Ops:
  7.2 760.7 %all-reduce.3.cloned.1.call-start = ((), (), s32[]{:S(2)}) async-start(), calls=%async_computation.3 | async-start | bytes 33554432
  480.3 0.7 copy-start
  480.3 421.1 %all-gather.2.cloned.1.call-start = ((), (), s32[]{:S(2)}) async-start(), calls=%async_computation.2 | async-start | bytes 20971520 | tf_op jit(solution)/shard_map/all_gather | solution.py:18
Sparse Core Ops, SparseCore 0:
  480.4 287.3 all-reduce.2
  795.5 105.9 all-gather.1
where the time goes:
time: 1330 us
  blocking collectives  741 us (56%)
  waiting for transfers between devices  392 us (29%)
  local copies, waits for them, and re-layouts  164 us (12%)
  between operations  14.7 us (1%)
  other arithmetic  13.9 us (1%)
    all_to_all x1, blocking collectives, on_device(): lax.all_to_all(local, 'fsdp', split_axis=2, concat_axis=1, tiled=True)  372 us
    all_to_all x1, blocking collectives, on_device(): lax.all_to_all(copies, 'fsdp', split_axis=1, concat_axis=2, tiled=True)  369 us
    unnamed x3, waiting for transfers between devices  286 us
    all_gather x1, waiting for transfers between devices, on_device(): copies = lax.all_gather(rounded, 'replica', axis=1, tiled=True)  106 us
    all_to_all x1, local copies, waits for them, and re-layouts, on_device(): lax.all_to_all(local, 'fsdp', split_axis=2, concat_axis=1, tiled=True)  60.3 us
    all_to_all x2, local copies, waits for them, and re-layouts, on_device(): lax.all_to_all(copies, 'fsdp', split_axis=1, concat_axis=2, tiled=True)  48.4 us
    unnamed x5, local copies, waits for them, and re-layouts  47 us
  transfers between devices with their start and end apart: 2, of which 2 were waited for; matrix products, arithmetic and copies ran while one was open for 0% of the time, Pallas kernels for 0%

commit v1 on v0

--- a/solution.py
+++ b/solution.py
@@ -15,7 +15,14 @@
     velocity = 0.9 * momentum + outer
     updated = master - 0.7 * (outer + 0.9 * velocity)
     rounded = updated.astype(jnp.bfloat16)
-    copies = lax.all_gather(rounded, "replica", axis=1, tiled=True)
+    ring = [rounded]
+    for hop in range(3):
+        ring.append(lax.ppermute(ring[-1], "replica", [(dev, (dev + 1) % 4) for dev in range(4)]))
+    copies = jnp.roll(
+        jnp.concatenate(ring[::-1], axis=1),
+        (lax.axis_index("replica") + 1) * ring[0].shape[1],
+        axis=1,
+    )
     spread = lax.all_to_all(copies, "fsdp", split_axis=1, concat_axis=2, tiled=True)
     return (updated, velocity, spread)
 

time: 1330 us -> 1450 us (1.090)
  local copies, waits for them, and re-layouts: 164 us -> 246 us
  waiting for transfers between devices: 392 us -> 430 us
    ppermute x0 -> x3, waiting for transfers between devices: none -> 144 us  [on_device(): lax.ppermute(ring[-1], 'replica', [(dev, (dev + 1) % 4) for dev in range(...]
    all_gather x1 -> x0, waiting for transfers between devices: 106 us -> none  [on_device(): copies = lax.all_gather(rounded, 'replica', axis=1, tiled=True)]
    dynamic_slice x0 -> x2, local copies, waits for them, and re-layouts: none -> 57.4 us  [on_device(): jnp.roll(jnp.concatenate(ring[::-1], axis=1), (lax.axis_index('replica')...]
    unnamed x5 -> x20, local copies, waits for them, and re-layouts: 47 us -> 77.6 us
    unnamed x3 -> x2, waiting for transfers between devices: 286 us -> 286 us
  transfers between devices with their start and end apart: 2 -> 4, of which waited for: 2 -> 4; matrix products, arithmetic and copies ran while one was open for 0% -> 0% of each run, Pallas kernels for 0% -> 0%
where the time goes in v1:
time: 1450 us; the launch traced here: 1440 us
  blocking collectives  739 us (51%)
  waiting for transfers between devices  430 us (30%)
  local copies, waits for them, and re-layouts  246 us (17%)
  between operations  14.7 us (1%)
    all_to_all x1, blocking collectives, on_device(): lax.all_to_all(local, 'fsdp', split_axis=2, concat_axis=1, tiled=True)  372 us
    all_to_all x1, blocking collectives, on_device(): lax.all_to_all(copies, 'fsdp', split_axis=1, concat_axis=2, tiled=True)  367 us
    unnamed x2, waiting for transfers between devices  286 us
    ppermute x3, waiting for transfers between devices, on_device(): lax.ppermute(ring[-1], 'replica', [(dev, (dev + 1) % 4) for dev in range(...  144 us
    unnamed x20, local copies, waits for them, and re-layouts  77.6 us
    all_to_all x1, local copies, waits for them, and re-layouts, on_device(): lax.all_to_all(local, 'fsdp', split_axis=2, concat_axis=1, tiled=True)  60.3 us
    dynamic_slice x2, local copies, waits for them, and re-layouts, on_device(): jnp.roll(jnp.concatenate(ring[::-1], axis=1), (lax.axis_index('replica')...  57.4 us
    all_to_all x2, local copies, waits for them, and re-layouts, on_device(): lax.all_to_all(copies, 'fsdp', split_axis=1, concat_axis=2, tiled=True)  48.4 us
  transfers between devices with their start and end apart: 4, of which 4 were waited for; matrix products, arithmetic and copies ran while one was open for 0% of the time, Pallas kernels for 0%

profile of v1, /device:TPU:0, one launch (start us, length us, event | category | flops | bytes accessed | tf_op | source)
XLA Modules:
  0.0 1441.9 jit_solution(3672924209705845874)
XLA Ops:
  7.2 0.0 all-reduce.3.cloned.1.call-start
  7.2 40.8 %copy.40 = bf16[1,2,256,16384]{2,1,3,0:T(2,128)(2,1)} copy(bf16[1,2,256,16384]{3,2,1,0:T(8,128)(2,1)} %param.3) | data formatting | bytes 33554432 | tf_op args[0]
  48.0 372.0 %all_to_all.36 = bf16[2,256,16384]{1,0,2:T(2,128)(2,1)} all-to-all(bf16[2,256,16384]{1,0,2:T(2,128)(2,1)} %bitcast.14), channel_id=1, replica_groups=mesh['replica'=4,'fsdp'=8] {'fsdp'}, dimensions={2} | all-to-all | bytes 33554432 | tf_op jit(solution)/shard_map/all_to_all | solution.py:10
  420.0 60.3 %copy.41 = bf16[2,8,256,2048]{3,0,2,1:T(2,128)(2,1)} copy(bf16[2,8,256,2048]{2,0,3,1:T(2,128)(2,1)} %bitcast.12) | data formatting | bytes 33554432 | tf_op jit(solution)/shard_map/all_to_all | solution.py:10
  480.4 0.0 copy-start.4
  480.4 0.0 all-reduce.3.cloned.1.call-update
  480.4 0.6 copy-done.4
  481.0 0.6 dynamic-slice
  482.2 285.6 %all-reduce.3.cloned.1.call-done = bf16[2,2048,2048]{2,0,1:T(2,128)(2,1)} async-done(((bf16[2,2048,2048]{2,0,1:T(2,128)(2,1)}), bf16[2,2048,2048]{2,0,1:T(2,128)(2,1)}) %all-reduce.3.cloned.1.call-update) | async-done | bytes 16777232
  767.9 5.1 constant_dynamic-slice_fusion
  773.0 12.5 fusion
  785.5 0.0 copy-start
  785.5 1.9 copy-done
  787.4 0.0 collective-permute-start
  787.4 47.9 %collective-permute-done = bf16[2,512,2048]{2,1,0:T(8,128)(2,1)S(1)} collective-permute-done((bf16[2,512,2048]{2,1,0:T(8,128)(2,1)S(1)}, bf16[2,512,2048]{2,1,0:T(8,128)(2,1)S(1)}, u32[]{:S(2)}, u32[]{:S(2)}) %collective-permute-start) | collective-permute-done | bytes 4194336 | tf_op jit(solution)/shard_map/ppermute | solution.py:20
  835.4 0.0 copy-start.2
  835.4 2.0 copy-done.2
  837.4 0.0 collective-permute-start.1
  837.4 48.0 %collective-permute-done.1 = bf16[2,512,2048]{2,1,0:T(8,128)(2,1)} collective-permute-done((bf16[2,512,2048]{2,1,0:T(8,128)(2,1)S(1)}, bf16[2,512,2048]{2,1,0:T(8,128)(2,1)}, u32[]{:S(2)}, u32[]{:S(2)}) %collective-permute-start.1) | collective-permute-done | bytes 4194336 | tf_op jit(solution)/shard_map/ppermute | solution.py:20
  885.4 0.0 collective-permute-start.2
  885.4 0.0 copy-start.3
  885.4 0.0 copy-start.1
  885.4 48.2 %collective-permute-done.2 = bf16[2,512,2048]{2,1,0:T(8,128)(2,1)} collective-permute-done((bf16[2,512,2048]{2,1,0:T(8,128)(2,1)}, bf16[2,512,2048]{2,1,0:T(8,128)(2,1)}, u32[]{:S(2)}, u32[]{:S(2)}) %collective-permute-start.2) | collective-permute-done | bytes 4194336 | tf_op jit(solution)/shard_map/ppermute | solution.py:20
  933.7 4.9 constant_dynamic-update-slice_fusion.7
  938.5 4.8 constant_dynamic-update-slice_fusion.6
  943.4 0.0 copy-done.3
  943.4 2.4 constant_dynamic-update-slice_fusion.5
  945.7 0.0 copy-done.1
  945.7 2.4 constant_dynamic-update-slice_fusion.4
  948.2 4.9 constant_dynamic-update-slice_fusion.3
  953.1 4.8 constant_dynamic-update-slice_fusion.2
  957.9 2.4 constant_dynamic-update-slice_fusion.1
  960.3 2.3 constant_dynamic-update-slice_fusion
  962.5 8.5 constant_dynamic-slice_fusion.1
  971.1 48.9 %copy.43 = bf16[2,2048,2048]{2,0,1:T(2,128)(2,1)} copy(bf16[2,2048,2048]{2,1,0:T(8,128)(2,1)S(1)} %constant_dynamic-slice_fusion.1) | data formatting | bytes 33554432 | tf_op jit(solution)/shard_map/jit(_roll_dynamic)/dynamic_slice | solution.py:21
  1019.9 366.7 %all_to_all.37 = bf16[2,2048,2048]{2,0,1:T(2,128)(2,1)S(1)} all-to-all(bf16[2,2048,2048]{2,0,1:T(2,128)(2,1)} %copy.43), channel_id=1, replica_groups=mesh['replica'=4,'fsdp'=8] {'fsdp'}, dimensions={1} | all-to-all | bytes 33554432 | tf_op jit(solution)/shard_map/all_to_all | solution.py:26
  1386.6 22.9 %copy.44 = bf16[2,256,8,2048]{3,2,1,0:T(8,128)(2,1)} copy(bf16[2,256,8,2048]{3,0,1,2:T(2,128)(2,1)S(1)} %bitcast.13) | data formatting | bytes 33554432 | tf_op jit(solution)/shard_map/all_to_all | solution.py:26
  1409.5 25.5 %all_to_all.33 = bf16[2,256,16384]{2,1,0:T(8,128)(2,1)} reshape(bf16[2,256,8,2048]{3,2,1,0:T(8,128)(2,1)} %copy.44) | data formatting | bytes 33554432 | tf_op jit(solution)/shard_map/all_to_all | solution.py:26
Async XLA Ops:
  7.2 760.7 %all-reduce.3.cloned.1.call-start = ((), (), s32[]{:S(2)}) async-start(), calls=%async_computation.2 | async-start | bytes 33554432
  480.4 0.7 copy-start.4
  785.5 1.9 copy-start
  787.4 47.9 %collective-permute-start = (bf16[2,512,2048]{2,1,0:T(8,128)(2,1)S(1)}, bf16[2,512,2048]{2,1,0:T(8,128)(2,1)S(1)}, u32[]{:S(2)}, u32[]{:S(2)}) collective-permute-start(bf16[2,512,2048]{2,1,0:T(8,128)(2,1)S(1)} %get-tuple-element.12), channel_id=1, source_target_pairs={{0,8},{8,16},{16,24},{24,0},{1,9},{9,17},{17,25},{25,1},{2,10},{10... | collective-permute-start | bytes 12582920 | tf_op jit(solution)/shard_map/ppermute | solution.py:20
  835.4 2.0 copy-start.2
  837.4 48.0 %collective-permute-start.1 = (bf16[2,512,2048]{2,1,0:T(8,128)(2,1)S(1)}, bf16[2,512,2048]{2,1,0:T(8,128)(2,1)}, u32[]{:S(2)}, u32[]{:S(2)}) collective-permute-start(bf16[2,512,2048]{2,1,0:T(8,128)(2,1)S(1)} %collective-permute-done), channel_id=1, source_target_pairs={{0,8},{8,16},{16,24},{24,0},{1,9},{9,17},{17,25},{25,1},{2,10},{10... | collective-permute-start | bytes 12582920 | tf_op jit(solution)/shard_map/ppermute | solution.py:20
  885.4 48.2 %collective-permute-start.2 = (bf16[2,512,2048]{2,1,0:T(8,128)(2,1)}, bf16[2,512,2048]{2,1,0:T(8,128)(2,1)}, u32[]{:S(2)}, u32[]{:S(2)}) collective-permute-start(bf16[2,512,2048]{2,1,0:T(8,128)(2,1)} %collective-permute-done.1), channel_id=1, source_target_pairs={{0,8},{8,16},{16,24},{24,0},{1,9},{9,17},{17,25},{25,1},{2,10},{10... | collective-permute-start | bytes 12582920 | tf_op jit(solution)/shard_map/ppermute | solution.py:20
  885.4 57.9 %copy-start.3 = (bf16[2,512,2048]{2,1,0:T(8,128)(2,1)S(1)}, bf16[2,512,2048]{2,1,0:T(8,128)(2,1)}, u32[]{:S(2)}) copy-start(bf16[2,512,2048]{2,1,0:T(8,128)(2,1)} %copy-done.2) | copy-start | bytes 12582916
  885.4 60.3 %copy-start.1 = (bf16[2,512,2048]{2,1,0:T(8,128)(2,1)S(1)}, bf16[2,512,2048]{2,1,0:T(8,128)(2,1)}, u32[]{:S(2)}) copy-start(bf16[2,512,2048]{2,1,0:T(8,128)(2,1)} %copy-done) | copy-start | bytes 12582916
Sparse Core Ops, SparseCore 0:
  480.5 287.3 all-reduce.2
